TPU v7x, 32 devices: a whole 2x2x4 slice. The times are simulated.
32 devices in a mesh: seq: 16 (over z, x, core), chan: 2 (over y).
Axes of the slice: x: 2, y: 2, z: 4, core: 2. Of those that a mesh axis runs over, the one named last changes fastest.
Arguments:
- inner_acts: bfloat16 [8192, 4096], P('seq', 'chan')
- gate_input: bfloat16 [8192, 4096], P('seq', 'chan'), may hold values from -6 to 6
- forward_keys: bfloat16 [8192, 128], P('seq'), may hold values from -0.5 to 0.5
- forward_queries: bfloat16 [8192, 128], P('seq'), may hold values from -6 to 6
- backward_keys: bfloat16 [8192, 128], P('seq'), may hold values from -0.5 to 0.5
- backward_queries: bfloat16 [8192, 128], P('seq'), may hold values from -6 to 6
- decay_codes: int32 [2, 32, 64], P(None, 'seq', 'chan'), may hold values from 1 to 24576
- clip_start: int32 [8192], P('seq'), may hold values 0 or 1
- skip_gain: float32 [64], P('chan'), may hold values from 0.3 to 3
- norm_gain: float32 [4096], P('chan'), may hold values from 0.1 to 1.9
- out_weight: bfloat16 [4096, 2048], P('chan'), may hold values from -0.09375 to 0.09375
Outputs:
- mixed: bfloat16 [2048, 2048], P('seq')
All inputs are finite; a program needn't handle non-finite values. No bound on the sum of `clip_start` on one device may be relied on, other than what follows from the above.
Results may differ from a plain program's by a relative error of at most 0.01.
Values may be sent and summed in bfloat16 or wider, within the bound.
No kernel may reach another device: no remote copies, remote signals or barrier semaphores. Data moves between devices by JAX's collectives and lax.ppermute only.
A program may use at most 128 MiB of HBM per device.

v0:
```python
import functools
import math

import jax
import jax.numpy as jnp
from jax import lax
from jax.experimental import pallas as pl
from jax.experimental.pallas import tpu as pltpu
from jax.sharding import PartitionSpec as P


POOL = 4
EPS = 1e-05
LOG2E = math.log2(math.e)
F32 = jnp.float32
BF16 = jnp.bfloat16


VM = pl.BlockSpec(memory_space=pltpu.VMEM)


def params(grid=True, mib=16):
    kw = {"dimension_semantics": ("arbitrary",)} if grid else {}
    return pltpu.CompilerParams(vmem_limit_bytes=mib * 1024 * 1024, **kw)


def vmem(x):
    return pltpu.with_memory_space_constraint(x, pltpu.VMEM)


def hbm(x):
    return pltpu.with_memory_space_constraint(x, pltpu.HBM)


def dot(a, b, dims=((1,), (0,)), precision=None):
    return lax.dot_general(a, b, (dims, ((), ())), precision=precision, preferred_element_type=F32)


def place():
    index = lax.axis_index("seq")
    block = index // 8
    return index % 2 == 1, (index // 2) % 4, block, 2 * (block % 2)


def lanes(start, count):
    return pl.ds(pl.multiple_of(start, 128), count)


def split_rows(v):
    high = v.astype(BF16)
    low = (v - high.astype(F32)).astype(BF16)
    return jnp.concatenate([high, low, jnp.zeros((6, v.shape[1]), BF16)], axis=0)


def joined(ref, nstate, at=slice(None)):
    rows = ref[nstate : nstate + 8, at].astype(F32)
    return rows[0:1] + rows[1:2]


def token_masks(row):
    span = row.shape[1]
    rows = lax.broadcasted_iota(jnp.int32, (span, span), 0)
    cols = lax.broadcasted_iota(jnp.int32, (span, span), 1)
    seg = jnp.sum(jnp.where(cols <= rows, row, 0.0), axis=1, keepdims=True)
    count = jnp.sum(row, axis=1, keepdims=True)
    return seg, count, rows, cols


def local_kernel(total, size, x, kf, kb, codes, skip, clip, send, keep, midf, midb, rows, keys):
    spans = 2
    span = clip.shape[1] // spans
    block = x.shape[1]
    nstate = kf.shape[1]
    step = pl.program_id(0)
    own_f, _, _, _ = place()
    wholes = []
    for s in range(spans):
        at = slice(s * span, (s + 1) * span)
        row = clip[0:1, at].astype(F32)
        wholes.append(jnp.sum(row, axis=1, keepdims=True) == 0.0)

    @pl.when(step == 0)
    def _():
        for s in range(spans):
            at = slice(s * span, (s + 1) * span)
            seg, count, _, _ = token_masks(clip[0:1, at].astype(F32))
            keys[0, at, :] = jnp.where(seg == count, kf[at, :].astype(F32), 0.0).astype(BF16)
            keys[1, at, :] = jnp.where(seg == 0.0, kb[at, :].astype(F32), 0.0).astype(BF16)

    heads = codes.shape[1]
    table = jnp.concatenate([codes[...].astype(F32), skip[...], jnp.zeros((3, heads), F32)], axis=0)
    lane = lax.broadcasted_iota(jnp.int32, (heads, block), 1) + step * block
    pick = lax.broadcasted_iota(jnp.int32, (heads, block), 0) == lane // size
    wide = dot(table, jnp.where(pick, 1.0, 0.0), precision=lax.Precision.HIGHEST)
    rate = wide[0:4] * (1.0 / (32.0 * total))
    logd = jnp.log1p(-rate) * LOG2E
    scal = jnp.sqrt(rate * (2.0 - rate))

    pos = lax.broadcasted_iota(jnp.int32, (span, 1), 0).astype(F32)
    lf, lb, pf, pb, df, db = [], [], [], [], [], []
    for s in range(spans):
        at = slice(s * span, (s + 1) * span)
        acts = x[at, :].astype(F32)
        log_f, log_b = logd[s : s + 1], logd[2 + s : 3 + s]
        xs_f = (acts * (scal[s : s + 1] * jnp.exp2((span - 1.0 - pos) * log_f))).astype(BF16)
        xs_b = (acts * (scal[2 + s : 3 + s] * jnp.exp2(pos * log_b))).astype(BF16)
        lf.append(dot(keys[0, at, :], xs_f, ((0,), (0,))))
        lb.append(dot(keys[1, at, :], xs_b, ((0,), (0,))))
        d_f, d_b = jnp.exp2(span * log_f), jnp.exp2(span * log_b)
        df.append(d_f)
        db.append(d_b)
        pf.append(jnp.where(wholes[s], d_f, 0.0))
        pb.append(jnp.where(wholes[s], d_b, 0.0))
    loc_f = pf[1] * lf[0] + lf[1]
    loc_b = lb[0] + pb[0] * lb[1]
    here = lanes(step * block, block)
    all_f, all_b = pf[0] * pf[1], pb[0] * pb[1]
    send[0:nstate, here] = jnp.where(own_f, loc_b, loc_f).astype(BF16)
    send[nstate : nstate + 8, here] = split_rows(jnp.where(own_f, all_b, all_f))
    keep[:, here] = jnp.where(own_f, loc_f, loc_b)
    midf[:, here] = lf[0].astype(BF16)
    midb[:, here] = lb[1].astype(BF16)
    own = jnp.where(own_f, all_f, all_b)
    rows[0:8, here] = jnp.concatenate([own, own, pf[0], pb[1], df[0], df[1], db[0], db[1]], axis=0)
    rows[8:16, here] = jnp.concatenate([logd, scal], axis=0)
    rows[16:24, here] = jnp.concatenate([wide[4:5], wide[1:8]], axis=0)


def score_kernel(after, kf, kb, qf, qb, clip, scores, query):
    spans = 2
    span = clip.shape[1] // spans
    for s in range(spans):
        at = slice(s * span, (s + 1) * span)
        row = clip[0:1, at].astype(F32)
        seg, count, rows, cols = token_masks(row)
        upto = jnp.where(rows <= cols, 1.0, 0.0).astype(BF16)
        seg_row = dot(jnp.broadcast_to(row, (8, span)).astype(BF16), upto)[0:1, :]
        same = seg == seg_row
        sf = dot(qf[at, :], kf[at, :], ((1,), (1,)))
        sb = dot(qb[at, :], kb[at, :], ((1,), (1,)))
        scores[2 * s] = jnp.where(same & (cols <= rows), sf, 0.0).astype(BF16)
        scores[2 * s + 1] = jnp.where(same & (cols >= rows), sb, 0.0).astype(BF16)
        query[0, at, :] = jnp.where(seg == 0.0, qf[at, :].astype(F32), 0.0).astype(BF16)
        query[1, at, :] = jnp.where(seg == count, qb[at, :].astype(F32), 0.0).astype(BF16)


def inner_kernel(first, *refs):
    after, x, gate, rows, midf, midb, scores, query, weight, *refs = refs
    if first:
        yg, gf, gb, weight_out, sem = refs
    else:
        yg, gf, gb, weight_out, sem = refs[4:]
    spans = 2
    block = x.shape[1]
    span = scores.shape[1]
    step = pl.program_id(0)
    steps = pl.num_programs(0)
    height = weight.shape[0] // 2
    band = pl.ds(0 if first else height, height)
    fetch = pltpu.make_async_copy(weight.at[band], weight_out.at[band], sem)

    @pl.when(step == 0)
    def _():
        fetch.start()

    here = lanes((step + (0 if first else steps)) * block, block)
    p = rows[0:8, here]
    logd, scal = rows[8:12, here], rows[12:16, here]
    skip = rows[16:24, here][0:1]
    pos = lax.broadcasted_iota(jnp.int32, (span, 1), 0).astype(F32)
    for s in range(spans):
        at = slice(s * span, (s + 1) * span)
        log_f, log_b = logd[s : s + 1], logd[2 + s : 3 + s]
        d_f, d_b = p[4 + s : 5 + s], p[6 + s : 7 + s]
        acts = x[at, :].astype(F32)
        xs_f = (acts * (scal[s : s + 1] * jnp.exp2((span - 1.0 - pos) * log_f))).astype(BF16)
        xs_b = (acts * (scal[2 + s : 3 + s] * jnp.exp2(pos * log_b))).astype(BF16)
        z = gate[at, :].astype(F32)
        g = z / (1.0 + jnp.exp(-z))
        g_f = g * jnp.exp2((pos - (span - 1.0)) * log_f)
        g_b = g * jnp.exp2(-pos * log_b)
        y_f, y_b = dot(scores[2 * s], xs_f), dot(scores[2 * s + 1], xs_b)
        if s == 1:
            y_f = y_f + dot(query[0, at, :], (d_f * midf[:, here].astype(F32)).astype(BF16))
            d_f = d_f * p[2:3]
        else:
            y_b = y_b + dot(query[1, at, :], (d_b * midb[:, here].astype(F32)).astype(BF16))
            d_b = d_b * p[3:4]
        yg[at, here] = g_f * y_f + g_b * y_b + g * (skip * acts)
        gf[at, here] = (g_f * d_f).astype(BF16)
        gb[at, here] = (g_b * d_b).astype(BF16)

    @pl.when(step == steps - 1)
    def _():
        fetch.wait()


def chip_kernel(recv, keep, rows, mine, passes, *sends):
    nstate, part = mine.shape
    _, chip, _, flip = place()
    for k in range(4):
        at = lanes((chip ^ k ^ flip) * part, part)
        own = rows[0:8, at][0:1]
        state = own * recv[0:nstate, at].astype(F32) + keep[:, at]
        both = own * joined(recv, nstate, at)
        if k == 0:
            mine[...] = state
            passes[...] = jnp.broadcast_to(both, (8, part))
        else:
            sends[k - 1][0:nstate, :] = state.astype(BF16)
            sends[k - 1][nstate : nstate + 8, :] = split_rows(both)


def group_kernel(recv_a, recv_b, recv_c, mine, passes, _, total, states, decays):
    nstate = mine.shape[0]
    own_f, chip, _, _ = place()
    states[chip] = mine[...]
    decays[chip] = passes[...]
    for k, recv in enumerate((recv_a, recv_b, recv_c)):
        states[chip ^ (k + 1)] = recv[0:nstate, :].astype(F32)
        decays[chip ^ (k + 1)] = jnp.broadcast_to(joined(recv, nstate), passes.shape)
    first = jnp.where(own_f, 0, 3)
    state, keep = states[first], decays[first][0:1]
    for t in range(1, 4):
        j = jnp.where(own_f, t, 3 - t)
        d = decays[j][0:1]
        state = d * state + states[j]
        keep = keep * d
    total[0:nstate, :] = state.astype(BF16)
    total[nstate : nstate + 8, :] = split_rows(keep)


def join_kernel(mine, recv, total):
    nstate = mine.shape[0] - 8
    keep = joined(mine, nstate)
    total[0:nstate, :] = (mine[0:nstate, :].astype(F32) + keep * recv[0:nstate, :].astype(F32)).astype(BF16)
    total[nstate : nstate + 8, :] = split_rows(keep * joined(recv, nstate))


def entry_kernel(pair, recv, states, decays, _, entry, send_a, send_b, send_c, ahead):
    nstate = entry.shape[0]
    own_f, chip, block, _ = place()
    state = recv[0:nstate, :].astype(F32)
    if pair:
        state = jnp.where(own_f == (block == 1), state, 0.0)
    for t in range(4):
        j = jnp.where(own_f, t, 3 - t)
        ahead[j] = state
        if t < 3:
            state = decays[j][0:1] * state + states[j]
    for k, out in enumerate((entry, send_a, send_b, send_c)):
        out[...] = ahead[chip ^ k].astype(BF16)


def carry_kernel(pieces, tokens, last, *refs):
    count = len(pieces)
    own_refs, oth_refs, refs = refs[:count], refs[count : 2 * count], refs[2 * count :]
    yg, gf, gb, recv, query, gain, *refs = refs
    before = None if pieces[0] == 0 else refs.pop(0)
    gated, sums = refs[:count], refs[count]
    own_f, chip, _, flip = place()
    nstate, part = own_refs[0].shape
    at = slice(*tokens)
    rel = slice(0, tokens[1] - tokens[0])
    acc = jnp.zeros((tokens[1] - tokens[0], 128), F32) if before is None else before[at, :]
    for own_ref, oth_ref, out, piece in zip(own_refs, oth_refs, gated, pieces):
        here = lanes((chip ^ piece ^ flip) * part, part)
        own = joined(recv, nstate, here) * own_ref[...].astype(F32) + recv[0:nstate, here].astype(F32)
        oth = oth_ref[...].astype(F32)
        st_f, st_b = jnp.where(own_f, own, oth).astype(BF16), jnp.where(own_f, oth, own).astype(BF16)
        c_f = dot(query[0, at, :], st_f)
        c_b = dot(query[1, at, :], st_b)
        v = yg[at, here] + gf[at, here].astype(F32) * c_f + gb[at, here].astype(F32) * c_b
        out[rel, :] = (v * gain[0:1, here]).astype(BF16)
        sq = v * v
        for k in range(part // 128):
            acc = acc + sq[:, k * 128 : (k + 1) * 128]
    if last:
        ones = jnp.ones((8, 128), BF16)
        high = acc.astype(BF16)
        low = (acc - high.astype(F32)).astype(BF16)
        sums[...] = dot(ones, high, ((1,), (1,))) + dot(ones, low, ((1,), (1,)))
    else:
        sums[...] = acc


def early_kernel(pieces_a, pieces_b, pieces_c, pieces_d, weight, high, low):
    part = pieces_a.shape[1]
    _, chip, _, flip = place()
    total = None
    for k, ref in enumerate((pieces_a, pieces_b, pieces_c, pieces_d)):
        at = lanes((chip ^ k ^ flip) * part, part)
        term = dot(ref[...], weight[at, 0 : high.shape[1]])
        total = term if total is None else total + term
    high[...] = total.astype(BF16)
    low[...] = (total - high[...].astype(F32)).astype(BF16)


def first_kernel(width, own, other, tokens_high, tokens_low, out, pool_high, pool_low):
    rows, tokens = pool_high.shape
    inv = lax.rsqrt((own[0:1, :] + other[0:1, :]) / width + EPS) * (1.0 / POOL)
    group = lax.broadcasted_iota(jnp.int32, (rows, tokens), 0)
    token = lax.broadcasted_iota(jnp.int32, (rows, tokens), 1)
    pool = jnp.where(token // POOL == group, inv, 0.0)
    high = pool.astype(BF16)
    low = (pool - high.astype(F32)).astype(BF16)
    pool_high[...] = high
    pool_low[...] = low
    out[...] = (dot(high, tokens_high[...]) + dot(high, tokens_low[...]) + dot(low, tokens_high[...])).astype(BF16)


def pool_kernel(pieces_a, pieces_b, pieces_c, pieces_d, high, low, pooled):
    part = pieces_a.shape[1]
    _, chip, _, flip = place()
    for k, ref in enumerate((pieces_a, pieces_b, pieces_c, pieces_d)):
        at = lanes((chip ^ k ^ flip) * part, part)
        pooled[:, at] = (dot(high[...], ref[...]) + dot(low[...], ref[...])).astype(BF16)


def project_kernel(start, pooled, weight, out):
    out[...] = dot(pooled[...], weight[:, start : start + out.shape[1]]).astype(BF16)


def sum_kernel(mine, peer, *refs):
    refs[-1][...] = (mine[...].astype(F32) + peer[...].astype(F32)).astype(BF16)


def swap(x, axis, bit):
    size = lax.axis_size(axis)
    return lax.ppermute(x, axis, [(i, i ^ bit) for i in range(size)])


def hop(x, steps):
    size = lax.axis_size("seq")
    pairs = []
    for i in range(size):
        j = (i + 8 * steps if i % 2 == 1 else i - 8 * steps) ^ (4 * (steps % 2))
        if 0 <= j < size:
            pairs.append((i, j))
    return lax.ppermute(x, "seq", pairs)


def call(kernel, outs, *ins, scratch=()):
    return pl.pallas_call(
        kernel,
        in_specs=[VM] * len(ins),
        out_specs=[VM] * len(outs),
        out_shape=[pltpu.VMEM(*o) for o in outs],
        scratch_shapes=list(scratch),
        compiler_params=params(False),
    )(*[vmem(x) for x in ins])


def body(
    inner_acts,
    gate_input,
    forward_keys,
    forward_queries,
    backward_keys,
    backward_queries,
    decay_codes,
    clip_start,
    skip_gain,
    norm_gain,
    out_weight,
):
    tokens, channels = inner_acts.shape
    heads = skip_gain.shape[0]
    spans = decay_codes.shape[1]
    span = tokens // spans
    nstate = forward_keys.shape[1]
    model = out_weight.shape[1]
    chan = lax.axis_size("chan")
    part = channels // 4
    assert spans == 2

    codes = decay_codes.reshape(2 * spans, heads)
    clip = clip_start.reshape(1, tokens)
    skip = skip_gain.reshape(1, heads)
    gain = norm_gain.reshape(1, channels)

    block = min(512, channels // 2)
    steps = channels // block
    tile = lambda rows: pl.BlockSpec((rows, block), lambda i: (0, i))
    full = lambda x: pl.BlockSpec(x.shape, lambda i: (0, 0))
    vshape = pltpu.VMEM

    send, keep, midf, midb, rows = pl.pallas_call(
        functools.partial(local_kernel, float(lax.axis_size("seq") * tokens), channels // heads),
        grid=(steps,),
        in_specs=[tile(tokens), full(forward_keys), full(backward_keys), full(codes), full(skip), full(clip)],
        out_specs=[VM] * 5,
        out_shape=[
            vshape((nstate + 8, channels), BF16), vshape((nstate, channels), F32), vshape((nstate, channels), BF16),
            vshape((nstate, channels), BF16), vshape((24, channels), F32),
        ],
        scratch_shapes=[pltpu.VMEM((2, tokens, nstate), BF16)],
        compiler_params=params(),
        name="local",
    )(*[hbm(x) for x in (inner_acts, forward_keys, backward_keys, codes, skip, clip)])

    recv1 = swap(send, "seq", 1)
    packed = ((nstate + 8, part), BF16)
    mine, passes, *sends = call(
        chip_kernel, [((nstate, part), F32), ((8, part), F32)] + [packed] * 3, recv1, keep, rows
    )
    recv2 = [swap(x, "seq", 2 * k + 2) for k, x in enumerate(sends)]

    keys = [forward_keys, backward_keys, forward_queries, backward_queries]
    scores, query = call(
        score_kernel, [((2 * spans, span, span), BF16), ((2, tokens, nstate), BF16)], sends[0], *keys, clip
    )
    inner_shapes = [
        vshape((tokens, channels), F32), vshape((tokens, channels), BF16), vshape((tokens, channels), BF16),
        vshape(out_weight.shape, BF16),
    ]

    def inner(first, after, prior):
        off = 0 if first else steps // 2
        wide = pl.BlockSpec((tokens, block), lambda i: (0, i + off))
        return pl.pallas_call(
            functools.partial(inner_kernel, first),
            grid=(max(steps // 2, 1),),
            in_specs=[VM, wide, wide, VM, VM, VM, VM, VM, pl.BlockSpec(memory_space=pltpu.HBM)] + [VM] * len(prior),
            out_specs=[VM] * 4,
            out_shape=inner_shapes,
            input_output_aliases={9 + k: k for k in range(len(prior))},
            scratch_shapes=[pltpu.SemaphoreType.DMA],
            compiler_params=params(),
            cost_estimate=pl.CostEstimate(flops=2 * 10**9, transcendentals=0, bytes_accessed=8 * 2**20),
            name="inner",
        )(
            vmem(after), inner_acts, gate_input, *[vmem(v) for v in (rows, midf, midb, scores, query)], hbm(out_weight),
            *[vmem(v) for v in prior],
        )

    half_done = inner(True, sends[0], [])

    total, states, decays = call(
        group_kernel, [packed, ((4, nstate, part), F32), ((4, 8, part), F32)], *recv2, mine, passes, scores
    )
    yg, gf, gb, weight = inner(False, total, half_done)
    blocks = lax.axis_size("seq") // 8
    if blocks == 2:
        before = swap(total, "seq", 12)
    else:
        step = 1
        while step < blocks:
            (total,) = call(join_kernel, [packed], total, hop(total, step))
            step *= 2
        before = hop(total, 1)
    own = call(
        functools.partial(entry_kernel, blocks == 2), [((nstate, part), BF16)] * 4, before, states, decays, weight,
        scratch=[pltpu.VMEM((4, nstate, part), F32)],
    )
    arrived = [own[0]]
    for k, x in enumerate(own[1:]):
        arrived.append(swap(x, "seq", 2 * k + 2))
    own = arrived
    peer = []
    for x in own:
        peer.append(swap(x, "seq", 1))

    def carry(pieces, span_at, last, before):
        length = span_at[1] - span_at[0]
        sums = ((8, length), F32) if last else ((length, 128), F32)
        return call(
            functools.partial(carry_kernel, pieces, span_at, last), [((length, part), BF16)] * len(pieces) + [sums],
            *[own[k] for k in pieces], *[peer[k] for k in pieces], yg, gf, gb, recv1, query, gain, *before,
        )

    done_0, acc = carry((0,), (0, tokens), False, [])
    done_1, acc = carry((1,), (0, tokens), False, [acc])
    done_2, acc = carry((2,), (0, tokens), False, [acc])
    done_3, squares = carry((3,), (0, tokens), True, [acc])
    if chan == 2:
        others = swap(squares, "chan", 1)
    else:
        squares, others = lax.psum(squares, "chan"), jnp.zeros_like(squares)
    out_rows = tokens // POOL
    first = model // 4
    done = [done_0, done_1, done_2, done_3]
    tokens_high, tokens_low = call(early_kernel, [((tokens, first), BF16)] * 2, *done, weight)
    mixed, high, low = call(
        functools.partial(first_kernel, float(channels * chan)),
        [((out_rows, first), BF16), ((out_rows, tokens), BF16), ((out_rows, tokens), BF16)],
        squares, others, tokens_high, tokens_low,
    )
    (pooled,) = call(pool_kernel, [((out_rows, channels), BF16)], *done, high, low)
    chunks = [(0, first), (first, model - first), (model - first, model)]
    out = None
    for k, (start, stop) in enumerate(chunks):
        if k:
            (mixed,) = call(
                functools.partial(project_kernel, start), [((out_rows, stop - start), BF16)], pooled, weight
            )
        if chan == 2:
            others = swap(mixed, "chan", 1)
        else:
            mixed, others = lax.psum(mixed.astype(F32), "chan").astype(BF16), jnp.zeros_like(mixed)
        prior = [] if out is None else [out]
        share = pl.BlockSpec((out_rows, first), lambda i: (0, i))
        out = pl.pallas_call(
            sum_kernel,
            grid=(mixed.shape[1] // first,),
            in_specs=[share, share] + [pl.BlockSpec(memory_space=pl.ANY)] * len(prior),
            out_specs=pl.BlockSpec((out_rows, first), lambda i, at=start // first: (0, i + at)),
            out_shape=jax.ShapeDtypeStruct((out_rows, model), BF16),
            input_output_aliases={2: 0} if prior else {},
            compiler_params=params(),
            name="sum",
        )(vmem(mixed), vmem(others), *prior)
    return out


def solution(mesh):
    placed = (
        P("seq", "chan"),
        P("seq", "chan"),
        P("seq", None),
        P("seq", None),
        P("seq", None),
        P("seq", None),
        P(None, "seq", "chan"),
        P("seq"),
        P("chan"),
        P("chan"),
        P("chan", None),
    )
    return jax.shard_map(body, mesh=mesh, in_specs=placed, out_specs=P("seq", None), check_vma=False)
```

profile of v0, /device:TPU:0, one launch (start us, length us, event | category | flops | bytes accessed | tf_op | source)
XLA Modules:
  0.0 58.6 jit_solution(883175964840668937)
XLA Ops:
  0.0 5.3 %local.1 = (bf16[136,2048]{1,0:T(8,128)(2,1)S(1)}, f32[128,2048]{1,0:T(8,128)S(1)}, bf16[128,2048]{1,0:T(8,128)(2,1)S(1)}, bf16[128,2048]{1,0:T(8,128)(2,1)S(1)}, f32[24,2048]{1,0:T(8,128)S(1)}) custom-call(bf16[512,2048]{1,0:T(8,128)(2,1)} %refs_1_.3, bf16[512,128]{1,0:T(8,128)(2,1)} %kf.3, bf16[512,128]{1,0:T(8,128)(2,1)} %kb.3, s32[4,32]{1,0:T(4,128)} %bitcast.10, ...), custom_call_target="tpu_custom_call" | custom-call | tf_op jit(solution)/shard_map/local/pallas_call | solution.py:388
  5.9 1.6 %collective-permute-done.recv.refs_5_ = bf16[136,2048]{1,0:T(8,128)(2,1)S(1)} collective-permute-done((bf16[136,2048]{1,0:T(8,128)(2,1)S(1)}, bf16[136,2048]{1,0:T(8,128)(2,1)S(1)}, u32[]{:S(2)}, u32[]{:S(2)}) %collective-permute-start) | collective-permute-done | bytes 557088 | tf_op jit(solution)/shard_map/ppermute | solution.py:330
  7.7 2.9 %collective-permute-start.1 = (bf16[136,512]{1,0:T(8,128)(2,1)S(1)}, bf16[136,512]{1,0:T(8,128)(2,1)S(1)}, u32[]{:S(2)}, u32[]{:S(2)}) collective-permute-start(bf16[136,512]{1,0:T(8,128)(2,1)S(1)} %get-tuple-element.48.after.refs_0_), channel_id=1, source_target_pairs={{0,4},{2,6},{4,0},{6,2},{8,12},{10,14},{12,8},{14,10},{16,20},{18,... | collective-permute-start | bytes 417800 | tf_op jit(solution)/shard_map/ppermute | solution.py:330
  10.6 1.6 %collective-permute-start.2 = (bf16[136,512]{1,0:T(8,128)(2,1)S(1)}, bf16[136,512]{1,0:T(8,128)(2,1)S(1)}, u32[]{:S(2)}, u32[]{:S(2)}) collective-permute-start(bf16[136,512]{1,0:T(8,128)(2,1)S(1)} %get-tuple-element.49), channel_id=1, source_target_pairs={{0,8},{2,10},{4,12},{6,14},{8,0},{10,2},{12,4},{14,6},{16,24},{18,... | collective-permute-start | bytes 417800 | tf_op jit(solution)/shard_map/ppermute | solution.py:330
  12.6 3.1 %inner.2 = (f32[512,2048]{1,0:T(8,128)S(1)}, bf16[512,2048]{1,0:T(8,128)(2,1)S(1)}, bf16[512,2048]{1,0:T(8,128)(2,1)S(1)}, bf16[2048,2048]{1,0:T(8,128)(2,1)S(1)}) custom-call(bf16[136,512]{1,0:T(8,128)(2,1)S(1)} %get-tuple-element.48.after.refs_0_, bf16[512,2048]{1,0:T(8,128)(2,1)S(1)} %copy-done, bf16[512,2048]{1,0:T(8,128)(2,1)S(1)} %copy-done.1, ...), custom_call_target="tpu_custom_call" | custom-call | flops 2000000000 | bytes 8388608 | tf_op jit(solution)/shard_map/inner/pallas_call | solution.py:421
  15.7 1.5 %collective-permute-done.2.recv_b = bf16[136,512]{1,0:T(8,128)(2,1)S(1)} collective-permute-done((bf16[136,512]{1,0:T(8,128)(2,1)S(1)}, bf16[136,512]{1,0:T(8,128)(2,1)S(1)}, u32[]{:S(2)}, u32[]{:S(2)}) %collective-permute-start.2) | collective-permute-done | bytes 139296 | tf_op jit(solution)/shard_map/ppermute | solution.py:330
  17.1 1.7 %collective-permute-done.3.recv_c = bf16[136,512]{1,0:T(8,128)(2,1)S(1)} collective-permute-done((bf16[136,512]{1,0:T(8,128)(2,1)S(1)}, bf16[136,512]{1,0:T(8,128)(2,1)S(1)}, u32[]{:S(2)}, u32[]{:S(2)}) %collective-permute-start.3) | collective-permute-done | bytes 139296 | tf_op jit(solution)/shard_map/ppermute | solution.py:330
  19.0 3.8 %collective-permute-start.4 = (bf16[136,512]{1,0:T(8,128)(2,1)S(1)}, bf16[136,512]{1,0:T(8,128)(2,1)S(1)}, u32[]{:S(2)}, u32[]{:S(2)}) collective-permute-start(bf16[136,512]{1,0:T(8,128)(2,1)S(1)} %get-tuple-element.54.refs_0_), channel_id=1, source_target_pairs={{0,24},{2,26},{4,28},{6,30},{8,16},{10,18},{12,20},{14,22},{16,8},... | collective-permute-start | bytes 417800 | tf_op jit(solution)/shard_map/ppermute | solution.py:330
  22.8 3.1 %inner.3 = (f32[512,2048]{1,0:T(8,128)S(1)}, bf16[512,2048]{1,0:T(8,128)(2,1)S(1)}, bf16[512,2048]{1,0:T(8,128)(2,1)S(1)}, bf16[2048,2048]{1,0:T(8,128)(2,1)S(1)}) custom-call(bf16[136,512]{1,0:T(8,128)(2,1)S(1)} %get-tuple-element.54.refs_0_, ...), custom_call_target="tpu_custom_call", output_to_operand_aliasing={{0}: (9, {}), {1}: (10, {}), {2}: (11, {}), {3}: (12, {})} | custom-call | flops 2000000000 | bytes 8388608 | tf_op jit(solution)/shard_map/inner/pallas_call | solution.py:421
  26.2 1.7 %collective-permute-start.6 = (bf16[128,512]{1,0:T(8,128)(2,1)S(1)}, bf16[128,512]{1,0:T(8,128)(2,1)S(1)}, u32[]{:S(2)}, u32[]{:S(2)}) collective-permute-start(bf16[128,512]{1,0:T(8,128)(2,1)S(1)} %get-tuple-element.70), channel_id=1, source_target_pairs={{0,4},{2,6},{4,0},{6,2},{8,12},{10,14},{12,8},{14,10},{16,20},{18,... | collective-permute-start | bytes 393224 | tf_op jit(solution)/shard_map/ppermute | solution.py:330
  27.9 2.3 %collective-permute-start.8 = (bf16[128,512]{1,0:T(8,128)(2,1)S(1)}, bf16[128,512]{1,0:T(8,128)(2,1)S(1)}, u32[]{:S(2)}, u32[]{:S(2)}) collective-permute-start(bf16[128,512]{1,0:T(8,128)(2,1)S(1)} %get-tuple-element.73), channel_id=1, source_target_pairs={{0,8},{2,10},{4,12},{6,14},{8,0},{10,2},{12,4},{14,6},{16,24},{18,... | collective-permute-start | bytes 393224 | tf_op jit(solution)/shard_map/ppermute | solution.py:330
  30.3 0.9 %collective-permute-done.6.refs_0_ = bf16[128,512]{1,0:T(8,128)(2,1)S(1)} collective-permute-done((bf16[128,512]{1,0:T(8,128)(2,1)S(1)}, bf16[128,512]{1,0:T(8,128)(2,1)S(1)}, u32[]{:S(2)}, u32[]{:S(2)}) %collective-permute-start.6) | collective-permute-done | bytes 131104 | tf_op jit(solution)/shard_map/ppermute | solution.py:330
  31.2 3.2 %collective-permute-done.8.refs_0_ = bf16[128,512]{1,0:T(8,128)(2,1)S(1)} collective-permute-done((bf16[128,512]{1,0:T(8,128)(2,1)S(1)}, bf16[128,512]{1,0:T(8,128)(2,1)S(1)}, u32[]{:S(2)}, u32[]{:S(2)}) %collective-permute-start.8) | collective-permute-done | bytes 131104 | tf_op jit(solution)/shard_map/ppermute | solution.py:330
  34.4 1.7 %collective-permute-done.10.refs_0_ = bf16[128,512]{1,0:T(8,128)(2,1)S(1)} collective-permute-done((bf16[128,512]{1,0:T(8,128)(2,1)S(1)}, bf16[128,512]{1,0:T(8,128)(2,1)S(1)}, u32[]{:S(2)}, u32[]{:S(2)}) %collective-permute-start.10) | collective-permute-done | bytes 131104 | tf_op jit(solution)/shard_map/ppermute | solution.py:330
  38.1 0.8 %shard_map.116 = (bf16[512,512]{1,0:T(8,128)(2,1)S(1)}, f32[8,512]{1,0:T(8,128)S(1)}) custom-call(bf16[128,512]{1,0:T(8,128)(2,1)S(1)} %collective-permute-done.10.refs_0_, bf16[128,512]{1,0:T(8,128)(2,1)S(1)} %collective-permute-done.11.refs_1_, f32[512,2048]{1,0:T(8,128)S(1)} %get-tuple-element.66.refs_2_, ...), custom_call_target="tpu_custom_call" | custom-call | tf_op jit(solution)/shard_map/pallas_call | solution.py:344
  38.9 1.6 %collective-permute-start.12 = (f32[8,512]{1,0:T(8,128)S(1)}, f32[8,512]{1,0:T(8,128)S(1)}, u32[]{:S(2)}, u32[]{:S(2)}) collective-permute-start(f32[8,512]{1,0:T(8,128)S(1)} %get-tuple-element.79.own), channel_id=1, source_target_pairs={{0,1},{1,0},{2,3},{3,2},{4,5},{5,4},{6,7},{7,6},{8,9},{9,8},{10,11... | collective-permute-start | bytes 49160 | tf_op jit(solution)/shard_map/ppermute | solution.py:330
  40.5 1.2 %shard_map.117 = (bf16[512,512]{1,0:T(8,128)(2,1)S(1)}, bf16[512,512]{1,0:T(8,128)(2,1)S(1)}) custom-call(bf16[512,512]{1,0:T(8,128)(2,1)S(1)} %get-tuple-element.69.pieces_a, bf16[512,512]{1,0:T(8,128)(2,1)S(1)} %get-tuple-element.72.pieces_b, bf16[512,512]{1,0:T(8,128)(2,1)S(1)} %get-tuple-element.75.pieces_c, ...), custom_call_target="tpu_custom_call" | custom-call | tf_op jit(solution)/shard_map/pallas_call | solution.py:344
  41.8 0.9 %collective-permute-done.12.other = f32[8,512]{1,0:T(8,128)S(1)} collective-permute-done((f32[8,512]{1,0:T(8,128)S(1)}, f32[8,512]{1,0:T(8,128)S(1)}, u32[]{:S(2)}, u32[]{:S(2)}) %collective-permute-start.12) | collective-permute-done | bytes 16416 | tf_op jit(solution)/shard_map/ppermute | solution.py:330
  43.1 0.7 %shard_map.119.pooled = bf16[128,2048]{1,0:T(8,128)(2,1)S(1)} custom-call(bf16[512,512]{1,0:T(8,128)(2,1)S(1)} %get-tuple-element.69.pieces_a, bf16[512,512]{1,0:T(8,128)(2,1)S(1)} %get-tuple-element.72.pieces_b, bf16[512,512]{1,0:T(8,128)(2,1)S(1)} %get-tuple-element.75.pieces_c, bf16[512,512]{1,0:T(8,128)(2,1)S(1)} %get-tuple-element.78.pieces_d, ...), custom_call_target="tpu_custom_call" | custom-call | tf_op jit(solution)/shard_map/pallas_call | solution.py:344
  43.8 0.7 %shard_map.121.mine = bf16[128,1024]{1,0:T(8,128)(2,1)S(1)} custom-call(bf16[128,2048]{1,0:T(8,128)(2,1)S(1)} %shard_map.119.pooled, bf16[2048,2048]{1,0:T(8,128)(2,1)S(1)} %get-tuple-element.64._.weight), custom_call_target="tpu_custom_call" | custom-call | tf_op jit(solution)/shard_map/pallas_call | solution.py:344
  44.6 1.6 %collective-permute-start.14 = (bf16[128,1024]{1,0:T(8,128)(2,1)S(1)}, bf16[128,1024]{1,0:T(8,128)(2,1)S(1)}, u32[]{:S(2)}, u32[]{:S(2)}) collective-permute-start(bf16[128,1024]{1,0:T(8,128)(2,1)S(1)} %shard_map.121.mine), channel_id=1, source_target_pairs={{0,1},{1,0},{2,3},{3,2},{4,5},{5,4},{6,7},{7,6},{8,9},{9,8},{10,11... | collective-permute-start | bytes 786440 | tf_op jit(solution)/shard_map/ppermute | solution.py:330
  47.1 1.6 %collective-permute-start.13 = (bf16[128,512]{1,0:T(8,128)(2,1)S(1)}, bf16[128,512]{1,0:T(8,128)(2,1)S(1)}, u32[]{:S(2)}, u32[]{:S(2)}) collective-permute-start(bf16[128,512]{1,0:T(8,128)(2,1)S(1)} %shard_map.120.mine), channel_id=1, source_target_pairs={{0,1},{1,0},{2,3},{3,2},{4,5},{5,4},{6,7},{7,6},{8,9},{9,8},{10,11... | collective-permute-start | bytes 393224 | tf_op jit(solution)/shard_map/ppermute | solution.py:330
  48.7 7.7 %collective-permute-done.15.peer = bf16[128,512]{1,0:T(8,128)(2,1)S(1)} collective-permute-done((bf16[128,512]{1,0:T(8,128)(2,1)S(1)}, bf16[128,512]{1,0:T(8,128)(2,1)S(1)}, u32[]{:S(2)}, u32[]{:S(2)}) %collective-permute-start.15) | collective-permute-done | bytes 131104 | tf_op jit(solution)/shard_map/ppermute | solution.py:330
  57.1 0.8 %sum.4.refs_0_ = bf16[128,2048]{1,0:T(8,128)(2,1)} custom-call(bf16[128,1024]{1,0:T(8,128)(2,1)S(1)} %shard_map.121.mine, bf16[128,1024]{1,0:T(8,128)(2,1)S(1)} %collective-permute-done.14.peer, bf16[128,2048]{1,0:T(8,128)(2,1)} %sum.3.refs_0_), custom_call_target="tpu_custom_call", output_to_operand_aliasing={{}: (2, {})} | custom-call | tf_op jit(solution)/shard_map/sum/pallas_call | solution.py:503
  (43 shorter events, 6.5 us)
Async XLA Ops:
  0.0 12.2 %copy-start.7 = (s32[512]{0:T(512)S(1)}, s32[512]{0:T(512)}, u32[]{:S(2)}) copy-start(s32[512]{0:T(512)} %param.18) | copy-start | bytes 6148
  0.0 12.2 %copy-start.2 = (bf16[512,128]{1,0:T(8,128)(2,1)S(1)}, bf16[512,128]{1,0:T(8,128)(2,1)}, u32[]{:S(2)}) copy-start(bf16[512,128]{1,0:T(8,128)(2,1)} %kf.3) | copy-start | bytes 393220
  0.0 12.2 %copy-start.3 = (bf16[512,128]{1,0:T(8,128)(2,1)S(1)}, bf16[512,128]{1,0:T(8,128)(2,1)}, u32[]{:S(2)}) copy-start(bf16[512,128]{1,0:T(8,128)(2,1)} %kb.3) | copy-start | bytes 393220
  0.0 12.2 %copy-start.4 = (bf16[512,128]{1,0:T(8,128)(2,1)S(1)}, bf16[512,128]{1,0:T(8,128)(2,1)}, u32[]{:S(2)}) copy-start(bf16[512,128]{1,0:T(8,128)(2,1)} %qf.1) | copy-start | bytes 393220
  0.0 12.2 %copy-start.5 = (bf16[512,128]{1,0:T(8,128)(2,1)S(1)}, bf16[512,128]{1,0:T(8,128)(2,1)}, u32[]{:S(2)}) copy-start(bf16[512,128]{1,0:T(8,128)(2,1)} %qb.1) | copy-start | bytes 393220
  0.0 12.5 %copy-start = (bf16[512,2048]{1,0:T(8,128)(2,1)S(1)}, bf16[512,2048]{1,0:T(8,128)(2,1)}, u32[]{:S(2)}) copy-start(bf16[512,2048]{1,0:T(8,128)(2,1)} %refs_1_.3) | copy-start | bytes 6291460
  0.0 12.5 %copy-start.1 = (bf16[512,2048]{1,0:T(8,128)(2,1)S(1)}, bf16[512,2048]{1,0:T(8,128)(2,1)}, u32[]{:S(2)}) copy-start(bf16[512,2048]{1,0:T(8,128)(2,1)} %refs_2_.3) | copy-start | bytes 6291460
  5.3 2.2 %collective-permute-start = (bf16[136,2048]{1,0:T(8,128)(2,1)S(1)}, bf16[136,2048]{1,0:T(8,128)(2,1)S(1)}, u32[]{:S(2)}, u32[]{:S(2)}) collective-permute-start(bf16[136,2048]{1,0:T(8,128)(2,1)S(1)} %get-tuple-element.45), channel_id=1, source_target_pairs={{0,2},{2,0},{4,6},{6,4},{8,10},{10,8},{12,14},{14,12},{16,18},{18,... | collective-permute-start | bytes 1671176 | tf_op jit(solution)/shard_map/ppermute | solution.py:330
  7.7 8.0 %collective-permute-start.1 = (bf16[136,512]{1,0:T(8,128)(2,1)S(1)}, bf16[136,512]{1,0:T(8,128)(2,1)S(1)}, u32[]{:S(2)}, u32[]{:S(2)}) collective-permute-start(bf16[136,512]{1,0:T(8,128)(2,1)S(1)} %get-tuple-element.48.after.refs_0_), channel_id=1, source_target_pairs={{0,4},{2,6},{4,0},{6,2},{8,12},{10,14},{12,8},{14,10},{16,20},{18,... | collective-permute-start | bytes 417800 | tf_op jit(solution)/shard_map/ppermute | solution.py:330
  10.6 6.5 %collective-permute-start.2 = (bf16[136,512]{1,0:T(8,128)(2,1)S(1)}, bf16[136,512]{1,0:T(8,128)(2,1)S(1)}, u32[]{:S(2)}, u32[]{:S(2)}) collective-permute-start(bf16[136,512]{1,0:T(8,128)(2,1)S(1)} %get-tuple-element.49), channel_id=1, source_target_pairs={{0,8},{2,10},{4,12},{6,14},{8,0},{10,2},{12,4},{14,6},{16,24},{18,... | collective-permute-start | bytes 417800 | tf_op jit(solution)/shard_map/ppermute | solution.py:330
  12.2 6.7 %collective-permute-start.3 = (bf16[136,512]{1,0:T(8,128)(2,1)S(1)}, bf16[136,512]{1,0:T(8,128)(2,1)S(1)}, u32[]{:S(2)}, u32[]{:S(2)}) collective-permute-start(bf16[136,512]{1,0:T(8,128)(2,1)S(1)} %get-tuple-element.50), channel_id=1, source_target_pairs={{0,12},{2,14},{4,8},{6,10},{8,4},{10,6},{12,0},{14,2},{16,28},{18,... | collective-permute-start | bytes 417800 | tf_op jit(solution)/shard_map/ppermute | solution.py:330
  19.0 6.9 %collective-permute-start.4 = (bf16[136,512]{1,0:T(8,128)(2,1)S(1)}, bf16[136,512]{1,0:T(8,128)(2,1)S(1)}, u32[]{:S(2)}, u32[]{:S(2)}) collective-permute-start(bf16[136,512]{1,0:T(8,128)(2,1)S(1)} %get-tuple-element.54.refs_0_), channel_id=1, source_target_pairs={{0,24},{2,26},{4,28},{6,30},{8,16},{10,18},{12,20},{14,22},{16,8},... | collective-permute-start | bytes 417800 | tf_op jit(solution)/shard_map/ppermute | solution.py:330
  25.9 10.1 %copy-start.6 = (f32[2048]{0:T(1024)S(1)}, f32[2048]{0:T(1024)}, u32[]{:S(2)}) copy-start(f32[2048]{0:T(1024)} %param.20) | copy-start | bytes 24580
  26.2 5.0 %collective-permute-start.6 = (bf16[128,512]{1,0:T(8,128)(2,1)S(1)}, bf16[128,512]{1,0:T(8,128)(2,1)S(1)}, u32[]{:S(2)}, u32[]{:S(2)}) collective-permute-start(bf16[128,512]{1,0:T(8,128)(2,1)S(1)} %get-tuple-element.70), channel_id=1, source_target_pairs={{0,4},{2,6},{4,0},{6,2},{8,12},{10,14},{12,8},{14,10},{16,20},{18,... | collective-permute-start | bytes 393224 | tf_op jit(solution)/shard_map/ppermute | solution.py:330
  27.9 6.5 %collective-permute-start.8 = (bf16[128,512]{1,0:T(8,128)(2,1)S(1)}, bf16[128,512]{1,0:T(8,128)(2,1)S(1)}, u32[]{:S(2)}, u32[]{:S(2)}) collective-permute-start(bf16[128,512]{1,0:T(8,128)(2,1)S(1)} %get-tuple-element.73), channel_id=1, source_target_pairs={{0,8},{2,10},{4,12},{6,14},{8,0},{10,2},{12,4},{14,6},{16,24},{18,... | collective-permute-start | bytes 393224 | tf_op jit(solution)/shard_map/ppermute | solution.py:330
  30.1 5.9 %collective-permute-start.10 = (bf16[128,512]{1,0:T(8,128)(2,1)S(1)}, bf16[128,512]{1,0:T(8,128)(2,1)S(1)}, u32[]{:S(2)}, u32[]{:S(2)}) collective-permute-start(bf16[128,512]{1,0:T(8,128)(2,1)S(1)} %get-tuple-element.76), channel_id=1, source_target_pairs={{0,12},{2,14},{4,8},{6,10},{8,4},{10,6},{12,0},{14,2},{16,28},{18,... | collective-permute-start | bytes 393224 | tf_op jit(solution)/shard_map/ppermute | solution.py:330
  30.3 5.8 %collective-permute-start.5 = (bf16[128,512]{1,0:T(8,128)(2,1)S(1)}, bf16[128,512]{1,0:T(8,128)(2,1)S(1)}, u32[]{:S(2)}, u32[]{:S(2)}) collective-permute-start(bf16[128,512]{1,0:T(8,128)(2,1)S(1)} %get-tuple-element.65.refs_0_), channel_id=1, source_target_pairs={{0,2},{2,0},{4,6},{6,4},{8,10},{10,8},{12,14},{14,12},{16,18},{18,... | collective-permute-start | bytes 393224 | tf_op jit(solution)/shard_map/ppermute | solution.py:330
  31.2 5.6 %collective-permute-start.7 = (bf16[128,512]{1,0:T(8,128)(2,1)S(1)}, bf16[128,512]{1,0:T(8,128)(2,1)S(1)}, u32[]{:S(2)}, u32[]{:S(2)}) collective-permute-start(bf16[128,512]{1,0:T(8,128)(2,1)S(1)} %collective-permute-done.6.refs_0_), channel_id=1, source_target_pairs={{0,2},{2,0},{4,6},{6,4},{8,10},{10,8},{12,14},{14,12},{16,18},{18,... | collective-permute-start | bytes 393224 | tf_op jit(solution)/shard_map/ppermute | solution.py:330
  34.4 3.0 %collective-permute-start.9 = (bf16[128,512]{1,0:T(8,128)(2,1)S(1)}, bf16[128,512]{1,0:T(8,128)(2,1)S(1)}, u32[]{:S(2)}, u32[]{:S(2)}) collective-permute-start(bf16[128,512]{1,0:T(8,128)(2,1)S(1)} %collective-permute-done.8.refs_0_), channel_id=1, source_target_pairs={{0,2},{2,0},{4,6},{6,4},{8,10},{10,8},{12,14},{14,12},{16,18},{18,... | collective-permute-start | bytes 393224 | tf_op jit(solution)/shard_map/ppermute | solution.py:330
  36.1 2.1 %collective-permute-start.11 = (bf16[128,512]{1,0:T(8,128)(2,1)S(1)}, bf16[128,512]{1,0:T(8,128)(2,1)S(1)}, u32[]{:S(2)}, u32[]{:S(2)}) collective-permute-start(bf16[128,512]{1,0:T(8,128)(2,1)S(1)} %collective-permute-done.10.refs_0_), channel_id=1, source_target_pairs={{0,2},{2,0},{4,6},{6,4},{8,10},{10,8},{12,14},{14,12},{16,18},{18,... | collective-permute-start | bytes 393224 | tf_op jit(solution)/shard_map/ppermute | solution.py:330
  38.9 3.8 %collective-permute-start.12 = (f32[8,512]{1,0:T(8,128)S(1)}, f32[8,512]{1,0:T(8,128)S(1)}, u32[]{:S(2)}, u32[]{:S(2)}) collective-permute-start(f32[8,512]{1,0:T(8,128)S(1)} %get-tuple-element.79.own), channel_id=1, source_target_pairs={{0,1},{1,0},{2,3},{3,2},{4,5},{5,4},{6,7},{7,6},{8,9},{9,8},{10,11... | collective-permute-start | bytes 49160 | tf_op jit(solution)/shard_map/ppermute | solution.py:330
  44.6 12.5 %collective-permute-start.14 = (bf16[128,1024]{1,0:T(8,128)(2,1)S(1)}, bf16[128,1024]{1,0:T(8,128)(2,1)S(1)}, u32[]{:S(2)}, u32[]{:S(2)}) collective-permute-start(bf16[128,1024]{1,0:T(8,128)(2,1)S(1)} %shard_map.121.mine), channel_id=1, source_target_pairs={{0,1},{1,0},{2,3},{3,2},{4,5},{5,4},{6,7},{7,6},{8,9},{9,8},{10,11... | collective-permute-start | bytes 786440 | tf_op jit(solution)/shard_map/ppermute | solution.py:330
  46.2 10.2 %collective-permute-start.15 = (bf16[128,512]{1,0:T(8,128)(2,1)S(1)}, bf16[128,512]{1,0:T(8,128)(2,1)S(1)}, u32[]{:S(2)}, u32[]{:S(2)}) collective-permute-start(bf16[128,512]{1,0:T(8,128)(2,1)S(1)} %get-tuple-element.84.mine), channel_id=1, source_target_pairs={{0,1},{1,0},{2,3},{3,2},{4,5},{5,4},{6,7},{7,6},{8,9},{9,8},{10,11... | collective-permute-start | bytes 393224 | tf_op jit(solution)/shard_map/ppermute | solution.py:330
  47.1 10.8 %collective-permute-start.13 = (bf16[128,512]{1,0:T(8,128)(2,1)S(1)}, bf16[128,512]{1,0:T(8,128)(2,1)S(1)}, u32[]{:S(2)}, u32[]{:S(2)}) collective-permute-start(bf16[128,512]{1,0:T(8,128)(2,1)S(1)} %shard_map.120.mine), channel_id=1, source_target_pairs={{0,1},{1,0},{2,3},{3,2},{4,5},{5,4},{6,7},{7,6},{8,9},{9,8},{10,11... | collective-permute-start | bytes 393224 | tf_op jit(solution)/shard_map/ppermute | solution.py:330
where the time goes:
time: 58.8 us; the launch traced here: 58.6 us
  Pallas kernels  20.9 us (36%)
  waiting for transfers between devices  19.1 us (32%)
  starting transfers between devices  18.3 us (31%)
    ppermute x16, waiting for transfers between devices, swap(): return lax.ppermute(x, axis, [(i, i ^ bit) for i in range(size)])  19.1 us
    ppermute x16, starting transfers between devices, swap(): return lax.ppermute(x, axis, [(i, i ^ bit) for i in range(size)])  18.3 us
    pallas_call x13, Pallas kernels, call(): pl.pallas_call(kernel, in_specs=[VM] * len(ins), out_specs=[VM] * len(out...  7.28 us
    pallas_call x2, Pallas kernels, inner(): pl.pallas_call(functools.partial(inner_kernel, first), grid=(max(steps //...  6.15 us
    pallas_call x1, Pallas kernels, body(): pl.pallas_call(functools.partial(local_kernel, float(lax.axis_size('seq')...  5.31 us
    pallas_call x3, Pallas kernels, body(): pl.pallas_call(sum_kernel, grid=(mixed.shape[1] // first,), in_specs=[sha...  2.18 us
  transfers between devices with their start and end apart: 16, of which 8 were waited for; matrix products, arithmetic and copies ran while one was open for 0% of the time, Pallas kernels for 20%

commit v1 on v0

--- a/solution.py
+++ b/solution.py
@@ -66,64 +66,86 @@
     return seg, count, rows, cols
 
 
-def local_kernel(total, size, x, kf, kb, codes, skip, clip, send, keep, midf, midb, rows, keys):
+def local_kernel(total, size, block, *refs):
+    sources, refs = refs[:9], refs[9:]
+    send, keep, midf, midb, rows, x, gate, qf, qb, kf, kb, clip, skip, codes, keys, sems = refs
+    targets = (clip, kf, kb, codes, skip, x, gate, qf, qb)
     spans = 2
     span = clip.shape[1] // spans
-    block = x.shape[1]
+    channels = x.shape[1]
     nstate = kf.shape[1]
-    step = pl.program_id(0)
+    steps = channels // block
     own_f, _, _, _ = place()
+    copies = []
+    for source, target in zip(sources, targets):
+        parts = [slice(None)]
+        if target is x:
+            parts = [pl.ds(i * block, block) for i in range(steps)]
+        for part in parts:
+            copies.append(pltpu.make_async_copy(source.at[:, part], target.at[:, part], sems.at[len(copies)]))
+            copies[-1].start()
+    for k in range(5):
+        copies[k].wait()
+
     wholes = []
     for s in range(spans):
         at = slice(s * span, (s + 1) * span)
-        row = clip[0:1, at].astype(F32)
-        wholes.append(jnp.sum(row, axis=1, keepdims=True) == 0.0)
-
-    @pl.when(step == 0)
-    def _():
-        for s in range(spans):
-            at = slice(s * span, (s + 1) * span)
-            seg, count, _, _ = token_masks(clip[0:1, at].astype(F32))
-            keys[0, at, :] = jnp.where(seg == count, kf[at, :].astype(F32), 0.0).astype(BF16)
-            keys[1, at, :] = jnp.where(seg == 0.0, kb[at, :].astype(F32), 0.0).astype(BF16)
+        seg, count, _, _ = token_masks(clip[0:1, at].astype(F32))
+        keys[0, at, :] = jnp.where(seg == count, kf[at, :].astype(F32), 0.0).astype(BF16)
+        keys[1, at, :] = jnp.where(seg == 0.0, kb[at, :].astype(F32), 0.0).astype(BF16)
+        wholes.append(count == 0.0)
 
     heads = codes.shape[1]
     table = jnp.concatenate([codes[...].astype(F32), skip[...], jnp.zeros((3, heads), F32)], axis=0)
-    lane = lax.broadcasted_iota(jnp.int32, (heads, block), 1) + step * block
-    pick = lax.broadcasted_iota(jnp.int32, (heads, block), 0) == lane // size
+    lane = lax.broadcasted_iota(jnp.int32, (heads, channels), 1)
+    pick = lax.broadcasted_iota(jnp.int32, (heads, channels), 0) == lane // size
     wide = dot(table, jnp.where(pick, 1.0, 0.0), precision=lax.Precision.HIGHEST)
-    rate = wide[0:4] * (1.0 / (32.0 * total))
-    logd = jnp.log1p(-rate) * LOG2E
-    scal = jnp.sqrt(rate * (2.0 - rate))
-
-    pos = lax.broadcasted_iota(jnp.int32, (span, 1), 0).astype(F32)
-    lf, lb, pf, pb, df, db = [], [], [], [], [], []
-    for s in range(spans):
-        at = slice(s * span, (s + 1) * span)
-        acts = x[at, :].astype(F32)
-        log_f, log_b = logd[s : s + 1], logd[2 + s : 3 + s]
-        xs_f = (acts * (scal[s : s + 1] * jnp.exp2((span - 1.0 - pos) * log_f))).astype(BF16)
-        xs_b = (acts * (scal[2 + s : 3 + s] * jnp.exp2(pos * log_b))).astype(BF16)
-        lf.append(dot(keys[0, at, :], xs_f, ((0,), (0,))))
-        lb.append(dot(keys[1, at, :], xs_b, ((0,), (0,))))
-        d_f, d_b = jnp.exp2(span * log_f), jnp.exp2(span * log_b)
-        df.append(d_f)
-        db.append(d_b)
-        pf.append(jnp.where(wholes[s], d_f, 0.0))
-        pb.append(jnp.where(wholes[s], d_b, 0.0))
-    loc_f = pf[1] * lf[0] + lf[1]
-    loc_b = lb[0] + pb[0] * lb[1]
-    here = lanes(step * block, block)
-    all_f, all_b = pf[0] * pf[1], pb[0] * pb[1]
-    send[0:nstate, here] = jnp.where(own_f, loc_b, loc_f).astype(BF16)
-    send[nstate : nstate + 8, here] = split_rows(jnp.where(own_f, all_b, all_f))
-    keep[:, here] = jnp.where(own_f, loc_f, loc_b)
-    midf[:, here] = lf[0].astype(BF16)
-    midb[:, here] = lb[1].astype(BF16)
-    own = jnp.where(own_f, all_f, all_b)
-    rows[0:8, here] = jnp.concatenate([own, own, pf[0], pb[1], df[0], df[1], db[0], db[1]], axis=0)
-    rows[8:16, here] = jnp.concatenate([logd, scal], axis=0)
-    rows[16:24, here] = jnp.concatenate([wide[4:5], wide[1:8]], axis=0)
+    rate_all = wide[0:4] * (1.0 / (32.0 * total))
+    log_all = jnp.log1p(-rate_all) * LOG2E
+    scal_all = jnp.sqrt(rate_all * (2.0 - rate_all))
+    rows[8:16, :] = jnp.concatenate([log_all, scal_all], axis=0)
+    rows[16:24, :] = jnp.concatenate([wide[4:5], wide[1:8]], axis=0)
+
+    group = 16
+    count = span // group
+    near = lax.broadcasted_iota(jnp.int32, (group, 1), 0).astype(F32)
+    far = lax.broadcasted_iota(jnp.int32, (count, 1), 0).astype(F32) * group
+    for i in range(steps):
+        here = slice(i * block, (i + 1) * block)
+        logd, scal = log_all[:, here], scal_all[:, here]
+        copies[5 + i].wait()
+        lf, lb, pf, pb, df, db = [], [], [], [], [], []
+        for s in range(spans):
+            log_f, log_b = logd[s : s + 1], logd[2 + s : 3 + s]
+            near_f = scal[s : s + 1] * jnp.exp2((group - 1.0 - near) * log_f)
+            near_b = scal[2 + s : 3 + s] * jnp.exp2(near * log_b)
+            far_f = jnp.exp2((span - group - far) * log_f)
+            far_b = jnp.exp2(far * log_b)
+            xs_f, xs_b = [], []
+            for a in range(count):
+                acts = x[s * span + a * group : s * span + (a + 1) * group, here].astype(F32)
+                xs_f.append((acts * near_f * far_f[a : a + 1]).astype(BF16))
+                xs_b.append((acts * near_b * far_b[a : a + 1]).astype(BF16))
+            at = slice(s * span, (s + 1) * span)
+            lf.append(dot(keys[0, at, :], jnp.concatenate(xs_f, axis=0), ((0,), (0,))))
+            lb.append(dot(keys[1, at, :], jnp.concatenate(xs_b, axis=0), ((0,), (0,))))
+            d_f, d_b = jnp.exp2(span * log_f), jnp.exp2(span * log_b)
+            df.append(d_f)
+            db.append(d_b)
+            pf.append(jnp.where(wholes[s], d_f, 0.0))
+            pb.append(jnp.where(wholes[s], d_b, 0.0))
+        loc_f = pf[1] * lf[0] + lf[1]
+        loc_b = lb[0] + pb[0] * lb[1]
+        all_f, all_b = pf[0] * pf[1], pb[0] * pb[1]
+        send[0:nstate, here] = jnp.where(own_f, loc_b, loc_f).astype(BF16)
+        send[nstate : nstate + 8, here] = split_rows(jnp.where(own_f, all_b, all_f))
+        keep[:, here] = jnp.where(own_f, loc_f, loc_b)
+        midf[:, here] = lf[0].astype(BF16)
+        midb[:, here] = lb[1].astype(BF16)
+        own = jnp.where(own_f, all_f, all_b)
+        rows[0:8, here] = jnp.concatenate([own, own, pf[0], pb[1], df[0], df[1], db[0], db[1]], axis=0)
+    for copy in copies[5 + steps :]:
+        copy.wait()
 
 
 def score_kernel(after, kf, kb, qf, qb, clip, scores, query):
@@ -144,38 +166,38 @@
         query[1, at, :] = jnp.where(seg == count, qb[at, :].astype(F32), 0.0).astype(BF16)
 
 
-def inner_kernel(first, *refs):
+def inner_kernel(first, block, *refs):
     after, x, gate, rows, midf, midb, scores, query, weight, *refs = refs
     if first:
         yg, gf, gb, weight_out, sem = refs
     else:
         yg, gf, gb, weight_out, sem = refs[4:]
-    spans = 2
-    block = x.shape[1]
     span = scores.shape[1]
-    step = pl.program_id(0)
-    steps = pl.num_programs(0)
+    half = x.shape[1] // 2
     height = weight.shape[0] // 2
     band = pl.ds(0 if first else height, height)
     fetch = pltpu.make_async_copy(weight.at[band], weight_out.at[band], sem)
 
-    @pl.when(step == 0)
-    def _():
-        fetch.start()
-
-    here = lanes((step + (0 if first else steps)) * block, block)
+    fetch.start()
+    for i in range(half // block):
+        base = i * block + (0 if first else half)
+        inner_block(slice(base, base + block), span, x, gate, rows, midf, midb, scores, query, yg, gf, gb)
+    fetch.wait()
+
+
+def inner_block(here, span, x, gate, rows, midf, midb, scores, query, yg, gf, gb):
     p = rows[0:8, here]
     logd, scal = rows[8:12, here], rows[12:16, here]
     skip = rows[16:24, here][0:1]
     pos = lax.broadcasted_iota(jnp.int32, (span, 1), 0).astype(F32)
-    for s in range(spans):
+    for s in range(2):
         at = slice(s * span, (s + 1) * span)
         log_f, log_b = logd[s : s + 1], logd[2 + s : 3 + s]
         d_f, d_b = p[4 + s : 5 + s], p[6 + s : 7 + s]
-        acts = x[at, :].astype(F32)
+        acts = x[at, here].astype(F32)
         xs_f = (acts * (scal[s : s + 1] * jnp.exp2((span - 1.0 - pos) * log_f))).astype(BF16)
         xs_b = (acts * (scal[2 + s : 3 + s] * jnp.exp2(pos * log_b))).astype(BF16)
-        z = gate[at, :].astype(F32)
+        z = gate[at, here].astype(F32)
         g = z / (1.0 + jnp.exp(-z))
         g_f = g * jnp.exp2((pos - (span - 1.0)) * log_f)
         g_b = g * jnp.exp2(-pos * log_b)
@@ -189,10 +211,6 @@
         yg[at, here] = g_f * y_f + g_b * y_b + g * (skip * acts)
         gf[at, here] = (g_f * d_f).astype(BF16)
         gb[at, here] = (g_b * d_b).astype(BF16)
-
-    @pl.when(step == steps - 1)
-    def _():
-        fetch.wait()
 
 
 def chip_kernel(recv, keep, rows, mine, passes, *sends):
@@ -381,23 +399,27 @@
 
     block = min(512, channels // 2)
     steps = channels // block
-    tile = lambda rows: pl.BlockSpec((rows, block), lambda i: (0, i))
-    full = lambda x: pl.BlockSpec(x.shape, lambda i: (0, 0))
     vshape = pltpu.VMEM
 
-    send, keep, midf, midb, rows = pl.pallas_call(
-        functools.partial(local_kernel, float(lax.axis_size("seq") * tokens), channels // heads),
-        grid=(steps,),
-        in_specs=[tile(tokens), full(forward_keys), full(backward_keys), full(codes), full(skip), full(clip)],
-        out_specs=[VM] * 5,
+    sources = (clip, forward_keys, backward_keys, codes, skip, inner_acts, gate_input, forward_queries, backward_queries)
+    small = (tokens, nstate)
+    send, keep, midf, midb, rows, acts, gate, q_f, q_b, k_f, k_b, starts = pl.pallas_call(
+        functools.partial(local_kernel, float(lax.axis_size("seq") * tokens), channels // heads, block),
+        in_specs=[pl.BlockSpec(memory_space=pltpu.HBM)] * len(sources),
+        out_specs=[VM] * 12,
         out_shape=[
             vshape((nstate + 8, channels), BF16), vshape((nstate, channels), F32), vshape((nstate, channels), BF16),
-            vshape((nstate, channels), BF16), vshape((24, channels), F32),
+            vshape((nstate, channels), BF16), vshape((24, channels), F32), vshape((tokens, channels), BF16),
+            vshape((tokens, channels), BF16), vshape(small, BF16), vshape(small, BF16), vshape(small, BF16),
+            vshape(small, BF16), vshape((1, tokens), clip.dtype),
         ],
-        scratch_shapes=[pltpu.VMEM((2, tokens, nstate), BF16)],
-        compiler_params=params(),
+        scratch_shapes=[
+            pltpu.VMEM(skip.shape, skip.dtype), pltpu.VMEM(codes.shape, codes.dtype), pltpu.VMEM((2, tokens, nstate), BF16),
+            pltpu.SemaphoreType.DMA((len(sources) - 1 + steps,)),
+        ],
+        compiler_params=params(False),
         name="local",
-    )(*[hbm(x) for x in (inner_acts, forward_keys, backward_keys, codes, skip, clip)])
+    )(*[hbm(v) for v in sources])
 
     recv1 = swap(send, "seq", 1)
     packed = ((nstate + 8, part), BF16)
@@ -406,9 +428,9 @@
     )
     recv2 = [swap(x, "seq", 2 * k + 2) for k, x in enumerate(sends)]
 
-    keys = [forward_keys, backward_keys, forward_queries, backward_queries]
+    keys = [k_f, k_b, q_f, q_b]
     scores, query = call(
-        score_kernel, [((2 * spans, span, span), BF16), ((2, tokens, nstate), BF16)], sends[0], *keys, clip
+        score_kernel, [((2 * spans, span, span), BF16), ((2, tokens, nstate), BF16)], sends[0], *keys, starts
     )
     inner_shapes = [
         vshape((tokens, channels), F32), vshape((tokens, channels), BF16), vshape((tokens, channels), BF16),
@@ -416,21 +438,18 @@
     ]
 
     def inner(first, after, prior):
-        off = 0 if first else steps // 2
-        wide = pl.BlockSpec((tokens, block), lambda i: (0, i + off))
         return pl.pallas_call(
-            functools.partial(inner_kernel, first),
-            grid=(max(steps // 2, 1),),
-            in_specs=[VM, wide, wide, VM, VM, VM, VM, VM, pl.BlockSpec(memory_space=pltpu.HBM)] + [VM] * len(prior),
+            functools.partial(inner_kernel, first, block),
+            in_specs=[VM] * 8 + [pl.BlockSpec(memory_space=pltpu.HBM)] + [VM] * len(prior),
             out_specs=[VM] * 4,
             out_shape=inner_shapes,
             input_output_aliases={9 + k: k for k in range(len(prior))},
             scratch_shapes=[pltpu.SemaphoreType.DMA],
-            compiler_params=params(),
+            compiler_params=params(False),
             cost_estimate=pl.CostEstimate(flops=2 * 10**9, transcendentals=0, bytes_accessed=8 * 2**20),
             name="inner",
         )(
-            vmem(after), inner_acts, gate_input, *[vmem(v) for v in (rows, midf, midb, scores, query)], hbm(out_weight),
+            vmem(after), *[vmem(v) for v in (acts, gate, rows, midf, midb, scores, query)], hbm(out_weight),
             *[vmem(v) for v in prior],
         )
 

time: 58.8 us -> 57.5 us (0.978)
  waiting for transfers between devices: 19.1 us -> 16.9 us
  Pallas kernels: 20.9 us -> 22.6 us
  starting transfers between devices: 18.3 us -> 17.6 us
    pallas_call x2, Pallas kernels: 6.15 us -> 9.49 us  [inner(): pl.pallas_call(functools.partial(inner_kernel, first, block), in_specs=[V...]
    ppermute x16, waiting for transfers between devices: 19.1 us -> 16.9 us  [swap(): return lax.ppermute(x, axis, [(i, i ^ bit) for i in range(size)])]
    pallas_call x1, Pallas kernels: 5.31 us -> 3.6 us  [body(): pl.pallas_call(functools.partial(local_kernel, float(lax.axis_size('seq')...]
    ppermute x16, starting transfers between devices: 18.3 us -> 17.6 us  [swap(): return lax.ppermute(x, axis, [(i, i ^ bit) for i in range(size)])]
  transfers between devices with their start and end apart: 16 -> 16, of which waited for: 8 -> 7; matrix products, arithmetic and copies ran while one was open for 0% -> 0% of each run, Pallas kernels for 20% -> 26%
where the time goes in v1:
time: 57.5 us; the launch traced here: 57.3 us
  Pallas kernels  22.6 us (39%)
  starting transfers between devices  17.6 us (31%)
  waiting for transfers between devices  16.9 us (29%)
    ppermute x16, starting transfers between devices, swap(): return lax.ppermute(x, axis, [(i, i ^ bit) for i in range(size)])  17.6 us
    ppermute x16, waiting for transfers between devices, swap(): return lax.ppermute(x, axis, [(i, i ^ bit) for i in range(size)])  16.9 us
    pallas_call x2, Pallas kernels, inner(): pl.pallas_call(functools.partial(inner_kernel, first, block), in_specs=[V...  9.49 us
    pallas_call x13, Pallas kernels, call(): pl.pallas_call(kernel, in_specs=[VM] * len(ins), out_specs=[VM] * len(out...  7.32 us
    pallas_call x1, Pallas kernels, body(): pl.pallas_call(functools.partial(local_kernel, float(lax.axis_size('seq')...  3.6 us
    pallas_call x3, Pallas kernels, body(): pl.pallas_call(sum_kernel, grid=(mixed.shape[1] // first,), in_specs=[sha...  2.18 us
  transfers between devices with their start and end apart: 16, of which 7 were waited for; matrix products, arithmetic and copies ran while one was open for 0% of the time, Pallas kernels for 26%

profile of v1, /device:TPU:0, one launch (start us, length us, event | category | flops | bytes accessed | tf_op | source)
XLA Modules:
  0.0 57.3 jit_solution(15929593623914694119)
XLA Ops:
  0.0 3.6 %local.1 = (bf16[136,2048]{1,0:T(8,128)(2,1)S(1)}, f32[128,2048]{1,0:T(8,128)S(1)}, bf16[128,2048]{1,0:T(8,128)(2,1)S(1)}, bf16[128,2048]{1,0:T(8,128)(2,1)S(1)}...) custom-call(s32[1,512]{1,0:T(1,128)} %bitcast.8, ...), custom_call_target="tpu_custom_call" | custom-call | tf_op jit(solution)/shard_map/local/pallas_call | solution.py:406
  4.2 1.6 %collective-permute-done.recv.refs_5_ = bf16[136,2048]{1,0:T(8,128)(2,1)S(1)} collective-permute-done((bf16[136,2048]{1,0:T(8,128)(2,1)S(1)}, bf16[136,2048]{1,0:T(8,128)(2,1)S(1)}, u32[]{:S(2)}, u32[]{:S(2)}) %collective-permute-start) | collective-permute-done | bytes 557088 | tf_op jit(solution)/shard_map/ppermute | solution.py:348
  5.9 2.9 %collective-permute-start.1 = (bf16[136,512]{1,0:T(8,128)(2,1)S(1)}, bf16[136,512]{1,0:T(8,128)(2,1)S(1)}, u32[]{:S(2)}, u32[]{:S(2)}) collective-permute-start(bf16[136,512]{1,0:T(8,128)(2,1)S(1)} %get-tuple-element.55.after.refs_0_), channel_id=1, source_target_pairs={{0,4},{2,6},{4,0},{6,2},{8,12},{10,14},{12,8},{14,10},{16,20},{18,... | collective-permute-start | bytes 417800 | tf_op jit(solution)/shard_map/ppermute | solution.py:348
  8.8 1.6 %collective-permute-start.2 = (bf16[136,512]{1,0:T(8,128)(2,1)S(1)}, bf16[136,512]{1,0:T(8,128)(2,1)S(1)}, u32[]{:S(2)}, u32[]{:S(2)}) collective-permute-start(bf16[136,512]{1,0:T(8,128)(2,1)S(1)} %get-tuple-element.56), channel_id=1, source_target_pairs={{0,8},{2,10},{4,12},{6,14},{8,0},{10,2},{12,4},{14,6},{16,24},{18,... | collective-permute-start | bytes 417800 | tf_op jit(solution)/shard_map/ppermute | solution.py:348
  10.7 4.9 %inner.2 = (f32[512,2048]{1,0:T(8,128)S(1)}, bf16[512,2048]{1,0:T(8,128)(2,1)S(1)}, bf16[512,2048]{1,0:T(8,128)(2,1)S(1)}, bf16[2048,2048]{1,0:T(8,128)(2,1)S(1)}) custom-call(bf16[136,512]{1,0:T(8,128)(2,1)S(1)} %get-tuple-element.55.after.refs_0_, bf16[512,2048]{1,0:T(8,128)(2,1)S(1)} %get-tuple-element.69.refs_1_, ...), custom_call_target="tpu_custom_call" | custom-call | flops 2000000000 | bytes 8388608 | tf_op jit(solution)/shard_map/inner/pallas_call | solution.py:441
  15.7 1.4 %collective-permute-done.3.recv_c = bf16[136,512]{1,0:T(8,128)(2,1)S(1)} collective-permute-done((bf16[136,512]{1,0:T(8,128)(2,1)S(1)}, bf16[136,512]{1,0:T(8,128)(2,1)S(1)}, u32[]{:S(2)}, u32[]{:S(2)}) %collective-permute-start.3) | collective-permute-done | bytes 139296 | tf_op jit(solution)/shard_map/ppermute | solution.py:348
  17.3 3.8 %collective-permute-start.4 = (bf16[136,512]{1,0:T(8,128)(2,1)S(1)}, bf16[136,512]{1,0:T(8,128)(2,1)S(1)}, u32[]{:S(2)}, u32[]{:S(2)}) collective-permute-start(bf16[136,512]{1,0:T(8,128)(2,1)S(1)} %get-tuple-element.66.refs_0_), channel_id=1, source_target_pairs={{0,24},{2,26},{4,28},{6,30},{8,16},{10,18},{12,20},{14,22},{16,8},... | collective-permute-start | bytes 417800 | tf_op jit(solution)/shard_map/ppermute | solution.py:348
  21.1 4.6 %inner.3 = (f32[512,2048]{1,0:T(8,128)S(1)}, bf16[512,2048]{1,0:T(8,128)(2,1)S(1)}, bf16[512,2048]{1,0:T(8,128)(2,1)S(1)}, bf16[2048,2048]{1,0:T(8,128)(2,1)S(1)}) custom-call(bf16[136,512]{1,0:T(8,128)(2,1)S(1)} %get-tuple-element.66.refs_0_, ...), custom_call_target="tpu_custom_call", output_to_operand_aliasing={{0}: (9, {}), {1}: (10, {}), {2}: (11, {}), {3}: (12, {})} | custom-call | flops 2000000000 | bytes 8388608 | tf_op jit(solution)/shard_map/inner/pallas_call | solution.py:441
  25.9 1.5 %collective-permute-start.6 = (bf16[128,512]{1,0:T(8,128)(2,1)S(1)}, bf16[128,512]{1,0:T(8,128)(2,1)S(1)}, u32[]{:S(2)}, u32[]{:S(2)}) collective-permute-start(bf16[128,512]{1,0:T(8,128)(2,1)S(1)} %get-tuple-element.84), channel_id=1, source_target_pairs={{0,4},{2,6},{4,0},{6,2},{8,12},{10,14},{12,8},{14,10},{16,20},{18,... | collective-permute-start | bytes 393224 | tf_op jit(solution)/shard_map/ppermute | solution.py:348
  27.5 0.9 %collective-permute-start.8 = (bf16[128,512]{1,0:T(8,128)(2,1)S(1)}, bf16[128,512]{1,0:T(8,128)(2,1)S(1)}, u32[]{:S(2)}, u32[]{:S(2)}) collective-permute-start(bf16[128,512]{1,0:T(8,128)(2,1)S(1)} %get-tuple-element.87), channel_id=1, source_target_pairs={{0,8},{2,10},{4,12},{6,14},{8,0},{10,2},{12,4},{14,6},{16,24},{18,... | collective-permute-start | bytes 393224 | tf_op jit(solution)/shard_map/ppermute | solution.py:348
  28.4 1.1 %collective-permute-start.10 = (bf16[128,512]{1,0:T(8,128)(2,1)S(1)}, bf16[128,512]{1,0:T(8,128)(2,1)S(1)}, u32[]{:S(2)}, u32[]{:S(2)}) collective-permute-start(bf16[128,512]{1,0:T(8,128)(2,1)S(1)} %get-tuple-element.90), channel_id=1, source_target_pairs={{0,12},{2,14},{4,8},{6,10},{8,4},{10,6},{12,0},{14,2},{16,28},{18,... | collective-permute-start | bytes 393224 | tf_op jit(solution)/shard_map/ppermute | solution.py:348
  29.5 2.5 %collective-permute-done.6.refs_0_ = bf16[128,512]{1,0:T(8,128)(2,1)S(1)} collective-permute-done((bf16[128,512]{1,0:T(8,128)(2,1)S(1)}, bf16[128,512]{1,0:T(8,128)(2,1)S(1)}, u32[]{:S(2)}, u32[]{:S(2)}) %collective-permute-start.6) | collective-permute-done | bytes 131104 | tf_op jit(solution)/shard_map/ppermute | solution.py:348
  32.0 0.8 %collective-permute-done.8.refs_0_ = bf16[128,512]{1,0:T(8,128)(2,1)S(1)} collective-permute-done((bf16[128,512]{1,0:T(8,128)(2,1)S(1)}, bf16[128,512]{1,0:T(8,128)(2,1)S(1)}, u32[]{:S(2)}, u32[]{:S(2)}) %collective-permute-start.8) | collective-permute-done | bytes 131104 | tf_op jit(solution)/shard_map/ppermute | solution.py:348
  32.8 1.9 %collective-permute-done.10.refs_0_ = bf16[128,512]{1,0:T(8,128)(2,1)S(1)} collective-permute-done((bf16[128,512]{1,0:T(8,128)(2,1)S(1)}, bf16[128,512]{1,0:T(8,128)(2,1)S(1)}, u32[]{:S(2)}, u32[]{:S(2)}) %collective-permute-start.10) | collective-permute-done | bytes 131104 | tf_op jit(solution)/shard_map/ppermute | solution.py:348
  36.8 0.8 %shard_map.116 = (bf16[512,512]{1,0:T(8,128)(2,1)S(1)}, f32[8,512]{1,0:T(8,128)S(1)}) custom-call(bf16[128,512]{1,0:T(8,128)(2,1)S(1)} %collective-permute-done.10.refs_0_, bf16[128,512]{1,0:T(8,128)(2,1)S(1)} %collective-permute-done.11.refs_1_, f32[512,2048]{1,0:T(8,128)S(1)} %get-tuple-element.80.refs_2_, ...), custom_call_target="tpu_custom_call" | custom-call | tf_op jit(solution)/shard_map/pallas_call | solution.py:362
  37.6 1.5 %collective-permute-start.12 = (f32[8,512]{1,0:T(8,128)S(1)}, f32[8,512]{1,0:T(8,128)S(1)}, u32[]{:S(2)}, u32[]{:S(2)}) collective-permute-start(f32[8,512]{1,0:T(8,128)S(1)} %get-tuple-element.93.own), channel_id=1, source_target_pairs={{0,1},{1,0},{2,3},{3,2},{4,5},{5,4},{6,7},{7,6},{8,9},{9,8},{10,11... | collective-permute-start | bytes 49160 | tf_op jit(solution)/shard_map/ppermute | solution.py:348
  39.1 1.3 %shard_map.117 = (bf16[512,512]{1,0:T(8,128)(2,1)S(1)}, bf16[512,512]{1,0:T(8,128)(2,1)S(1)}) custom-call(bf16[512,512]{1,0:T(8,128)(2,1)S(1)} %get-tuple-element.83.pieces_a, bf16[512,512]{1,0:T(8,128)(2,1)S(1)} %get-tuple-element.86.pieces_b, bf16[512,512]{1,0:T(8,128)(2,1)S(1)} %get-tuple-element.89.pieces_c, ...), custom_call_target="tpu_custom_call" | custom-call | tf_op jit(solution)/shard_map/pallas_call | solution.py:362
  40.4 1.0 %collective-permute-done.12.other = f32[8,512]{1,0:T(8,128)S(1)} collective-permute-done((f32[8,512]{1,0:T(8,128)S(1)}, f32[8,512]{1,0:T(8,128)S(1)}, u32[]{:S(2)}, u32[]{:S(2)}) %collective-permute-start.12) | collective-permute-done | bytes 16416 | tf_op jit(solution)/shard_map/ppermute | solution.py:348
  41.8 0.7 %shard_map.119.pooled = bf16[128,2048]{1,0:T(8,128)(2,1)S(1)} custom-call(bf16[512,512]{1,0:T(8,128)(2,1)S(1)} %get-tuple-element.83.pieces_a, bf16[512,512]{1,0:T(8,128)(2,1)S(1)} %get-tuple-element.86.pieces_b, bf16[512,512]{1,0:T(8,128)(2,1)S(1)} %get-tuple-element.89.pieces_c, bf16[512,512]{1,0:T(8,128)(2,1)S(1)} %get-tuple-element.92.pieces_d, ...), custom_call_target="tpu_custom_call" | custom-call | tf_op jit(solution)/shard_map/pallas_call | solution.py:362
  42.5 0.7 %shard_map.121.mine = bf16[128,1024]{1,0:T(8,128)(2,1)S(1)} custom-call(bf16[128,2048]{1,0:T(8,128)(2,1)S(1)} %shard_map.119.pooled, bf16[2048,2048]{1,0:T(8,128)(2,1)S(1)} %get-tuple-element.78._.weight), custom_call_target="tpu_custom_call" | custom-call | tf_op jit(solution)/shard_map/pallas_call | solution.py:362
  43.3 1.6 %collective-permute-start.14 = (bf16[128,1024]{1,0:T(8,128)(2,1)S(1)}, bf16[128,1024]{1,0:T(8,128)(2,1)S(1)}, u32[]{:S(2)}, u32[]{:S(2)}) collective-permute-start(bf16[128,1024]{1,0:T(8,128)(2,1)S(1)} %shard_map.121.mine), channel_id=1, source_target_pairs={{0,1},{1,0},{2,3},{3,2},{4,5},{5,4},{6,7},{7,6},{8,9},{9,8},{10,11... | collective-permute-start | bytes 786440 | tf_op jit(solution)/shard_map/ppermute | solution.py:348
  45.8 1.6 %collective-permute-start.13 = (bf16[128,512]{1,0:T(8,128)(2,1)S(1)}, bf16[128,512]{1,0:T(8,128)(2,1)S(1)}, u32[]{:S(2)}, u32[]{:S(2)}) collective-permute-start(bf16[128,512]{1,0:T(8,128)(2,1)S(1)} %shard_map.120.mine), channel_id=1, source_target_pairs={{0,1},{1,0},{2,3},{3,2},{4,5},{5,4},{6,7},{7,6},{8,9},{9,8},{10,11... | collective-permute-start | bytes 393224 | tf_op jit(solution)/shard_map/ppermute | solution.py:348
  47.4 7.7 %collective-permute-done.15.peer = bf16[128,512]{1,0:T(8,128)(2,1)S(1)} collective-permute-done((bf16[128,512]{1,0:T(8,128)(2,1)S(1)}, bf16[128,512]{1,0:T(8,128)(2,1)S(1)}, u32[]{:S(2)}, u32[]{:S(2)}) %collective-permute-start.15) | collective-permute-done | bytes 131104 | tf_op jit(solution)/shard_map/ppermute | solution.py:348
  55.8 0.8 %sum.4.refs_0_ = bf16[128,2048]{1,0:T(8,128)(2,1)} custom-call(bf16[128,1024]{1,0:T(8,128)(2,1)S(1)} %shard_map.121.mine, bf16[128,1024]{1,0:T(8,128)(2,1)S(1)} %collective-permute-done.14.peer, bf16[128,2048]{1,0:T(8,128)(2,1)} %sum.3.refs_0_), custom_call_target="tpu_custom_call", output_to_operand_aliasing={{}: (2, {})} | custom-call | tf_op jit(solution)/shard_map/sum/pallas_call | solution.py:522
  (29 shorter events, 6.3 us)
Async XLA Ops:
  3.6 2.1 %collective-permute-start = (bf16[136,2048]{1,0:T(8,128)(2,1)S(1)}, bf16[136,2048]{1,0:T(8,128)(2,1)S(1)}, u32[]{:S(2)}, u32[]{:S(2)}) collective-permute-start(bf16[136,2048]{1,0:T(8,128)(2,1)S(1)} %get-tuple-element.52), channel_id=1, source_target_pairs={{0,2},{2,0},{4,6},{6,4},{8,10},{10,8},{12,14},{14,12},{16,18},{18,... | collective-permute-start | bytes 1671176 | tf_op jit(solution)/shard_map/ppermute | solution.py:348
  5.9 9.7 %collective-permute-start.1 = (bf16[136,512]{1,0:T(8,128)(2,1)S(1)}, bf16[136,512]{1,0:T(8,128)(2,1)S(1)}, u32[]{:S(2)}, u32[]{:S(2)}) collective-permute-start(bf16[136,512]{1,0:T(8,128)(2,1)S(1)} %get-tuple-element.55.after.refs_0_), channel_id=1, source_target_pairs={{0,4},{2,6},{4,0},{6,2},{8,12},{10,14},{12,8},{14,10},{16,20},{18,... | collective-permute-start | bytes 417800 | tf_op jit(solution)/shard_map/ppermute | solution.py:348
  8.8 6.8 %collective-permute-start.2 = (bf16[136,512]{1,0:T(8,128)(2,1)S(1)}, bf16[136,512]{1,0:T(8,128)(2,1)S(1)}, u32[]{:S(2)}, u32[]{:S(2)}) collective-permute-start(bf16[136,512]{1,0:T(8,128)(2,1)S(1)} %get-tuple-element.56), channel_id=1, source_target_pairs={{0,8},{2,10},{4,12},{6,14},{8,0},{10,2},{12,4},{14,6},{16,24},{18,... | collective-permute-start | bytes 417800 | tf_op jit(solution)/shard_map/ppermute | solution.py:348
  10.4 6.7 %collective-permute-start.3 = (bf16[136,512]{1,0:T(8,128)(2,1)S(1)}, bf16[136,512]{1,0:T(8,128)(2,1)S(1)}, u32[]{:S(2)}, u32[]{:S(2)}) collective-permute-start(bf16[136,512]{1,0:T(8,128)(2,1)S(1)} %get-tuple-element.57), channel_id=1, source_target_pairs={{0,12},{2,14},{4,8},{6,10},{8,4},{10,6},{12,0},{14,2},{16,28},{18,... | collective-permute-start | bytes 417800 | tf_op jit(solution)/shard_map/ppermute | solution.py:348
  17.3 8.4 %collective-permute-start.4 = (bf16[136,512]{1,0:T(8,128)(2,1)S(1)}, bf16[136,512]{1,0:T(8,128)(2,1)S(1)}, u32[]{:S(2)}, u32[]{:S(2)}) collective-permute-start(bf16[136,512]{1,0:T(8,128)(2,1)S(1)} %get-tuple-element.66.refs_0_), channel_id=1, source_target_pairs={{0,24},{2,26},{4,28},{6,30},{8,16},{10,18},{12,20},{14,22},{16,8},... | collective-permute-start | bytes 417800 | tf_op jit(solution)/shard_map/ppermute | solution.py:348
  25.7 9.0 %copy-start = (f32[2048]{0:T(1024)S(1)}, f32[2048]{0:T(1024)}, u32[]{:S(2)}) copy-start(f32[2048]{0:T(1024)} %param.20) | copy-start | bytes 24580
  25.9 6.0 %collective-permute-start.6 = (bf16[128,512]{1,0:T(8,128)(2,1)S(1)}, bf16[128,512]{1,0:T(8,128)(2,1)S(1)}, u32[]{:S(2)}, u32[]{:S(2)}) collective-permute-start(bf16[128,512]{1,0:T(8,128)(2,1)S(1)} %get-tuple-element.84), channel_id=1, source_target_pairs={{0,4},{2,6},{4,0},{6,2},{8,12},{10,14},{12,8},{14,10},{16,20},{18,... | collective-permute-start | bytes 393224 | tf_op jit(solution)/shard_map/ppermute | solution.py:348
  27.5 5.3 %collective-permute-start.8 = (bf16[128,512]{1,0:T(8,128)(2,1)S(1)}, bf16[128,512]{1,0:T(8,128)(2,1)S(1)}, u32[]{:S(2)}, u32[]{:S(2)}) collective-permute-start(bf16[128,512]{1,0:T(8,128)(2,1)S(1)} %get-tuple-element.87), channel_id=1, source_target_pairs={{0,8},{2,10},{4,12},{6,14},{8,0},{10,2},{12,4},{14,6},{16,24},{18,... | collective-permute-start | bytes 393224 | tf_op jit(solution)/shard_map/ppermute | solution.py:348
  28.4 6.3 %collective-permute-start.10 = (bf16[128,512]{1,0:T(8,128)(2,1)S(1)}, bf16[128,512]{1,0:T(8,128)(2,1)S(1)}, u32[]{:S(2)}, u32[]{:S(2)}) collective-permute-start(bf16[128,512]{1,0:T(8,128)(2,1)S(1)} %get-tuple-element.90), channel_id=1, source_target_pairs={{0,12},{2,14},{4,8},{6,10},{8,4},{10,6},{12,0},{14,2},{16,28},{18,... | collective-permute-start | bytes 393224 | tf_op jit(solution)/shard_map/ppermute | solution.py:348
  29.5 5.2 %collective-permute-start.5 = (bf16[128,512]{1,0:T(8,128)(2,1)S(1)}, bf16[128,512]{1,0:T(8,128)(2,1)S(1)}, u32[]{:S(2)}, u32[]{:S(2)}) collective-permute-start(bf16[128,512]{1,0:T(8,128)(2,1)S(1)} %get-tuple-element.79.refs_0_), channel_id=1, source_target_pairs={{0,2},{2,0},{4,6},{6,4},{8,10},{10,8},{12,14},{14,12},{16,18},{18,... | collective-permute-start | bytes 393224 | tf_op jit(solution)/shard_map/ppermute | solution.py:348
  32.0 3.4 %collective-permute-start.7 = (bf16[128,512]{1,0:T(8,128)(2,1)S(1)}, bf16[128,512]{1,0:T(8,128)(2,1)S(1)}, u32[]{:S(2)}, u32[]{:S(2)}) collective-permute-start(bf16[128,512]{1,0:T(8,128)(2,1)S(1)} %collective-permute-done.6.refs_0_), channel_id=1, source_target_pairs={{0,2},{2,0},{4,6},{6,4},{8,10},{10,8},{12,14},{14,12},{16,18},{18,... | collective-permute-start | bytes 393224 | tf_op jit(solution)/shard_map/ppermute | solution.py:348
  32.8 3.3 %collective-permute-start.9 = (bf16[128,512]{1,0:T(8,128)(2,1)S(1)}, bf16[128,512]{1,0:T(8,128)(2,1)S(1)}, u32[]{:S(2)}, u32[]{:S(2)}) collective-permute-start(bf16[128,512]{1,0:T(8,128)(2,1)S(1)} %collective-permute-done.8.refs_0_), channel_id=1, source_target_pairs={{0,2},{2,0},{4,6},{6,4},{8,10},{10,8},{12,14},{14,12},{16,18},{18,... | collective-permute-start | bytes 393224 | tf_op jit(solution)/shard_map/ppermute | solution.py:348
  34.7 2.1 %collective-permute-start.11 = (bf16[128,512]{1,0:T(8,128)(2,1)S(1)}, bf16[128,512]{1,0:T(8,128)(2,1)S(1)}, u32[]{:S(2)}, u32[]{:S(2)}) collective-permute-start(bf16[128,512]{1,0:T(8,128)(2,1)S(1)} %collective-permute-done.10.refs_0_), channel_id=1, source_target_pairs={{0,2},{2,0},{4,6},{6,4},{8,10},{10,8},{12,14},{14,12},{16,18},{18,... | collective-permute-start | bytes 393224 | tf_op jit(solution)/shard_map/ppermute | solution.py:348
  37.6 3.8 %collective-permute-start.12 = (f32[8,512]{1,0:T(8,128)S(1)}, f32[8,512]{1,0:T(8,128)S(1)}, u32[]{:S(2)}, u32[]{:S(2)}) collective-permute-start(f32[8,512]{1,0:T(8,128)S(1)} %get-tuple-element.93.own), channel_id=1, source_target_pairs={{0,1},{1,0},{2,3},{3,2},{4,5},{5,4},{6,7},{7,6},{8,9},{9,8},{10,11... | collective-permute-start | bytes 49160 | tf_op jit(solution)/shard_map/ppermute | solution.py:348
  43.3 12.5 %collective-permute-start.14 = (bf16[128,1024]{1,0:T(8,128)(2,1)S(1)}, bf16[128,1024]{1,0:T(8,128)(2,1)S(1)}, u32[]{:S(2)}, u32[]{:S(2)}) collective-permute-start(bf16[128,1024]{1,0:T(8,128)(2,1)S(1)} %shard_map.121.mine), channel_id=1, source_target_pairs={{0,1},{1,0},{2,3},{3,2},{4,5},{5,4},{6,7},{7,6},{8,9},{9,8},{10,11... | collective-permute-start | bytes 786440 | tf_op jit(solution)/shard_map/ppermute | solution.py:348
  44.8 10.3 %collective-permute-start.15 = (bf16[128,512]{1,0:T(8,128)(2,1)S(1)}, bf16[128,512]{1,0:T(8,128)(2,1)S(1)}, u32[]{:S(2)}, u32[]{:S(2)}) collective-permute-start(bf16[128,512]{1,0:T(8,128)(2,1)S(1)} %get-tuple-element.98.mine), channel_id=1, source_target_pairs={{0,1},{1,0},{2,3},{3,2},{4,5},{5,4},{6,7},{7,6},{8,9},{9,8},{10,11... | collective-permute-start | bytes 393224 | tf_op jit(solution)/shard_map/ppermute | solution.py:348
  45.8 10.8 %collective-permute-start.13 = (bf16[128,512]{1,0:T(8,128)(2,1)S(1)}, bf16[128,512]{1,0:T(8,128)(2,1)S(1)}, u32[]{:S(2)}, u32[]{:S(2)}) collective-permute-start(bf16[128,512]{1,0:T(8,128)(2,1)S(1)} %shard_map.120.mine), channel_id=1, source_target_pairs={{0,1},{1,0},{2,3},{3,2},{4,5},{5,4},{6,7},{7,6},{8,9},{9,8},{10,11... | collective-permute-start | bytes 393224 | tf_op jit(solution)/shard_map/ppermute | solution.py:348
